TPU v7x, 32 devices: a whole 2x2x4 slice. The times are simulated.
32 devices in a mesh: rows: 2 (over x), cols: 8 (over z, y), frames: 2 (over core).
Axes of the slice: x: 2, y: 2, z: 4, core: 2. Of those that a mesh axis runs over, the one named last changes fastest.
Arguments:
- lidar_map: bfloat16 [8, 96, 192, 256], P('frames', ('rows', 'cols')), parts along dimension 0, may hold values from -6 to 6
- camera_map: bfloat16 [8, 96, 192, 80], P('frames', None, ('rows', 'cols')), parts along dimension 0, may hold values from -6 to 6
- joined_weight: bfloat16 [3, 3, 336, 256], replicated, may hold values from -0.15625 to 0.15625
- joined_bias: float32 [256], replicated, may hold values from -0.5 to 0.5
- block_weight: bfloat16 [3, 3, 256, 128], replicated, may hold values from -0.1875 to 0.1875
- block_bias: float32 [128], replicated, may hold values from -0.5 to 0.5
- down_weight: bfloat16 [3, 3, 128, 256], replicated, may hold values from -0.25 to 0.25
- down_bias: float32 [256], replicated, may hold values from -0.5 to 0.5
- proj_weight: bfloat16 [256, 128], replicated, may hold values from -0.5 to 0.5
- proj_bias: float32 [128], replicated, may hold values from -0.5 to 0.5
Outputs:
- encoded: bfloat16 [8, 96, 192, 256], P('frames', 'rows', 'cols'), parts along dimension 0
There are 2 independent parts, one for each index of `frames`. A program takes and returns all parts, laid end to end along the dimension named above; an argument that names none is the same for every part. Nothing has to cross between parts.
All inputs are finite; a program needn't handle non-finite values.
Results may differ from a plain program's by a relative error of at most 0.0058.
Values may be sent and summed in bfloat16 or wider, within the bound.
A program may use at most 64 MiB of HBM per device.

v0:
```python
import functools

import jax
import jax.numpy as jnp
from jax import lax
from jax.experimental import pallas as pl
from jax.experimental.pallas import tpu as pltpu
from jax.sharding import PartitionSpec as P

MESH = pl.DeviceIdType.MESH
ABOVE, BELOW = 3, 2


def exchange_kernel(
    R, C, lidar, cam, tile, cams,
    l_send, l_recv, l_own, c_send, c_recv, h_send, h_recv,
):
    frames, strip, _, _ = lidar.shape
    blocks = cams.shape[0]
    width = tile.shape[2]
    height = strip * C
    r, c = lax.axis_index("rows"), lax.axis_index("cols")
    me = r * C + c
    n = R * C

    barrier = pltpu.get_barrier_semaphore()

    @pl.loop(1, n)
    def _(k):
        other = lax.rem(me + k, n)
        pl.semaphore_signal(
            barrier, inc=1,
            device_id={"rows": other // C, "cols": lax.rem(other, C)},
            device_id_type=MESH,
        )

    pl.semaphore_wait(barrier, n - 1)

    def lidar_copy(f, k):
        to = lax.rem(c + k, C)
        return pltpu.make_async_remote_copy(
            src_ref=lidar.at[f, :, pl.ds(pl.multiple_of(to * width, 8), width), :],
            dst_ref=tile.at[f, pl.ds(ABOVE + c * strip, strip)],
            send_sem=l_send.at[f, k], recv_sem=l_recv.at[f, k],
            device_id={"cols": to}, device_id_type=MESH,
        )

    def lidar_arrival(f, k):
        by = lax.rem(c + C - k, C)
        ref = tile.at[f, pl.ds(ABOVE + by * strip, strip)]
        return pltpu.make_async_copy(ref, ref, l_recv.at[f, k])

    def own_copy(f):
        return pltpu.make_async_copy(
            lidar.at[f, :, pl.ds(pl.multiple_of(c * width, 8), width), :],
            tile.at[f, pl.ds(ABOVE + c * strip, strip)],
            l_own.at[f],
        )

    to_col, slot = me // blocks, lax.rem(me, blocks)

    def cam_refs(f, row):
        return (
            cam.at[f, pl.ds(row * height, height)],
            cams.at[slot, f, pl.ds(ABOVE, height)],
        )

    def cam_remote(f, row):
        src, dst = cam_refs(f, row)
        return pltpu.make_async_remote_copy(
            src_ref=src, dst_ref=dst,
            send_sem=c_send.at[f, row], recv_sem=c_recv.at[f, slot],
            device_id={"rows": row, "cols": to_col}, device_id_type=MESH,
        )

    def cam_local(f, row):
        src, dst = cam_refs(f, row)
        return pltpu.make_async_copy(src, dst, c_recv.at[f, slot])

    def cam_arrival(f, b):
        ref = cams.at[b, f, pl.ds(ABOVE, height)]
        return pltpu.make_async_copy(ref, ref, c_recv.at[f, b])

    def here(row):
        return jnp.logical_and(row == r, to_col == c)

    for f in range(frames):
        for row in range(R):
            @pl.when(jnp.logical_not(here(row)))
            def _():
                cam_remote(f, row).start()

            @pl.when(here(row))
            def _():
                cam_local(f, row).start()

        for k in range(1, C):
            lidar_copy(f, k).start()
        own_copy(f).start()

    @pl.when(r == 0)
    def _():
        tile[:, 0:ABOVE] = jnp.zeros((frames, ABOVE) + tile.shape[2:], tile.dtype)
        cams[:, :, 0:ABOVE] = jnp.zeros((blocks, frames, ABOVE) + cams.shape[3:], cams.dtype)

    @pl.when(r == R - 1)
    def _():
        tile[:, ABOVE + height:] = jnp.zeros((frames, BELOW) + tile.shape[2:], tile.dtype)
        cams[:, :, ABOVE + height:] = jnp.zeros(
            (blocks, frames, BELOW) + cams.shape[3:], cams.dtype
        )

    def rims(f, down):
        src, dst, size = (height, 0, ABOVE) if down else (ABOVE, ABOVE + height, BELOW)
        row = r + 1 if down else r - 1
        way = 0 if down else 1
        pairs = [(tile.at[f, pl.ds(src, size)], tile.at[f, pl.ds(dst, size)])]
        pairs += [
            (cams.at[b, f, pl.ds(src, size)], cams.at[b, f, pl.ds(dst, size)])
            for b in range(blocks)
        ]
        return [
            pltpu.make_async_remote_copy(
                src_ref=a, dst_ref=z,
                send_sem=h_send.at[f, way, i], recv_sem=h_recv.at[f, way, i],
                device_id={"rows": row}, device_id_type=MESH,
            )
            for i, (a, z) in enumerate(pairs)
        ]

    for f in range(frames):
        own_copy(f).wait()
        for k in range(1, C):
            lidar_arrival(f, k).wait()
        for b in range(blocks):
            cam_arrival(f, b).wait()

        @pl.when(r < R - 1)
        def _():
            for copy in rims(f, True):
                copy.start()

        @pl.when(r > 0)
        def _():
            for copy in rims(f, False):
                copy.start()

    for f in range(frames):
        @pl.when(r < R - 1)
        def _():
            for copy in rims(f, True):
                copy.wait_send()
            for copy in rims(f, False):
                copy.wait_recv()

        @pl.when(r > 0)
        def _():
            for copy in rims(f, False):
                copy.wait_send()
            for copy in rims(f, True):
                copy.wait_recv()

        for k in range(1, C):
            lidar_copy(f, k).wait_send()
        for row in range(R):
            @pl.when(jnp.logical_not(here(row)))
            def _():
                cam_remote(f, row).wait_send()


def exchange(lidar_map, camera_map):
    R, C = lax.axis_size("rows"), lax.axis_size("cols")
    frames, strip, grid_width, channels = lidar_map.shape
    _, _, cam_width, cam_channels = camera_map.shape
    height, width = strip * C, grid_width // C
    blocks = width // cam_width
    packed = cam_width * cam_channels
    lanes = max(d for d in range(1, 129) if packed % d == 0)
    cam = camera_map.reshape(frames, R * height, packed // lanes, lanes)
    rows = ABOVE + height + BELOW
    dma = pltpu.SemaphoreType.DMA
    tile, cams = pl.pallas_call(
        functools.partial(exchange_kernel, R, C),
        out_shape=(
            jax.ShapeDtypeStruct((frames, rows, width, channels), lidar_map.dtype),
            jax.ShapeDtypeStruct((blocks, frames, rows) + cam.shape[2:], cam.dtype),
        ),
        in_specs=[pl.BlockSpec(memory_space=pl.ANY)] * 2,
        out_specs=[pl.BlockSpec(memory_space=pltpu.VMEM)] * 2,
        scratch_shapes=[
            dma((frames, C)), dma((frames, C)), dma((frames,)),
            dma((frames, R)), dma((frames, blocks)),
            dma((frames, 2, 1 + blocks)), dma((frames, 2, 1 + blocks)),
        ],
        compiler_params=pltpu.CompilerParams(collective_id=0, has_side_effects=True),
    )(lidar_map, cam)
    cams = cams.reshape(blocks, frames, rows, cam_width, cam_channels)
    cams = cams.transpose(1, 2, 0, 3, 4).reshape(frames, rows, width, cam_channels)
    return jnp.concatenate([tile, cams], axis=-1)


def conv_valid(inputs, kernel, stride):
    return lax.conv_general_dilated(
        inputs,
        kernel,
        (stride, stride),
        "VALID",
        dimension_numbers=("NHWC", "HWIO", "NHWC"),
        preferred_element_type=jnp.float32,
    )


def inside(values, above, left, height, width):
    R, C = lax.axis_size("rows"), lax.axis_size("cols")
    row = lax.axis_index("rows") * height - above + jnp.arange(values.shape[1])
    col = lax.axis_index("cols") * width - left + jnp.arange(values.shape[2])
    rows_in = (row >= 0) & (row < R * height)
    cols_in = (col >= 0) & (col < C * width)
    return jnp.where((rows_in[:, None] & cols_in[None, :])[None, :, :, None], values, 0)


def local(
    lidar_map,
    camera_map,
    joined_weight,
    joined_bias,
    block_weight,
    block_bias,
    down_weight,
    down_bias,
    proj_weight,
    proj_bias,
):
    C = lax.axis_size("cols")
    height, width = lidar_map.shape[1] * C, lidar_map.shape[2] // C
    stacked = exchange(lidar_map, camera_map)
    right = [(i, i + 1) for i in range(C - 1)]
    left = [(i + 1, i) for i in range(C - 1)]
    padded = jnp.concatenate(
        [
            lax.ppermute(stacked[:, :, -ABOVE:], "cols", right),
            stacked,
            lax.ppermute(stacked[:, :, :BELOW], "cols", left),
        ],
        axis=2,
    )
    joined = jax.nn.relu(conv_valid(padded, joined_weight, 1) + joined_bias).astype(jnp.bfloat16)
    joined = inside(joined, 2, 2, height, width)
    block = jax.nn.relu(conv_valid(joined, block_weight, 1) + block_bias).astype(jnp.bfloat16)
    block = inside(block, 1, 1, height, width)
    deep = jax.nn.relu(conv_valid(block, down_weight, 2) + down_bias).astype(jnp.bfloat16)
    branch = jax.nn.relu(
        jnp.einsum("fijc,cd->fijd", deep, proj_weight, preferred_element_type=jnp.float32)
        + proj_bias
    ).astype(jnp.bfloat16)
    upsampled = jnp.repeat(jnp.repeat(branch, 2, axis=1), 2, axis=2)
    return jnp.concatenate([block[:, 1:, 1:], upsampled], axis=-1)


def solution(mesh):
    return jax.shard_map(
        local,
        mesh=mesh,
        in_specs=(
            P("frames", ("rows", "cols"), None, None),
            P("frames", None, ("rows", "cols"), None),
        ) + (P(),) * 8,
        out_specs=P("frames", "rows", "cols", None),
        check_vma=False,
    )
```

profile of v0, /device:TPU:14, one launch (start us, length us, event | category | flops | bytes accessed | tf_op | source)
XLA Modules:
  0.0 220.2 jit_solution(9224455712384875803)
XLA Ops:
  0.0 2.4 %copy.30.cam = bf16[4,96,8,120]{3,2,1,0:T(8,128)(2,1)} copy(bf16[4,96,8,120]{1,3,2,0:T(8,128)(2,1)} %bitcast.54) | data formatting | bytes 1474560 | tf_op jit(solution)/shard_map/reshape | solution.py:179
  2.4 95.5 %shard_map.100 = (bf16[4,53,24,256]{3,2,1,0:T(8,128)(2,1)}, bf16[2,4,53,8,120]{4,3,2,1,0:T(8,128)(2,1)}) custom-call(bf16[4,6,192,256]{3,2,1,0:T(8,128)(2,1)} %lidar.1, bf16[4,96,8,120]{3,2,1,0:T(8,128)(2,1)} %copy.30.cam), custom_call_target="tpu_custom_call" | custom-call | tf_op jit(solution)/shard_map/pallas_call | solution.py:182
  97.9 3.5 %constant_dynamic-update-slice_fusion = bf16[4,53,24,336]{3,2,1,0:T(8,128)(2,1)} fusion(bf16[4,53,24,256]{3,2,1,0:T(8,128)(2,1)} %get-tuple-element.7), kind=kLoop, calls=%fused_computation.36 | loop fusion | bytes 5210112
  101.4 2.7 %reshape.110 = bf16[2,4,53,12,80]{4,3,2,1,0:T(8,128)(2,1)S(1)} reshape(bf16[2,4,53,8,120]{4,3,2,1,0:T(8,128)(2,1)} %get-tuple-element.8) | data formatting | bytes 1628160 | tf_op jit(solution)/shard_map/reshape | solution.py:197
  104.1 0.4 copy.31
  104.4 1.3 copy_dynamic-update-slice_fusion
  105.7 1.7 slice.18
  107.4 0.2 copy.33
  107.6 1.9 collective-permute-start
  109.5 1.5 slice.19
  111.0 3.9 %collective-permute-start.1 = (bf16[4,53,2,336]{3,2,1,0:T(2,128)(2,1)S(1)}, bf16[4,53,2,336]{3,2,1,0:T(2,128)(2,1)S(1)}, u32[]{:S(2)}, u32[]{:S(2)}) collective-permute-start(bf16[4,53,2,336]{3,2,1,0:T(2,128)(2,1)S(1)} %slice.19), channel_id=1, source_target_pairs={{2,0},{4,2},{6,4},{8,6},{10,8},{12,10},{14,12},{3,1},{5,3},{7,5},{... | collective-permute-start | bytes 854792 | tf_op jit(solution)/shard_map/ppermute | solution.py:243
  115.0 0.1 broadcast_and_fusion
  115.1 0.1 broadcast_and_fusion.1
  115.2 13.5 %collective-permute-done = bf16[4,53,3,336]{3,0,2,1:T(4,128)(2,1)S(1)} collective-permute-done((bf16[4,53,3,336]{3,0,2,1:T(4,128)(2,1)S(1)}, bf16[4,53,3,336]{3,0,2,1:T(4,128)(2,1)S(1)}, u32[]{:S(2)}, u32[]{:S(2)}) %collective-permute-start) | collective-permute-done | bytes 427424 | tf_op jit(solution)/shard_map/ppermute | solution.py:241
  128.7 0.3 copy.34
  129.0 5.0 %maximum_bitcast_fusion = bf16[53,4,29,336]{3,2,0,1:T(8,128)(2,1)S(1)} fusion(bf16[4,53,2,336]{3,2,1,0:T(2,128)(2,1)S(1)} %collective-permute-done.1, bf16[4,53,24,336]{3,2,1,0:T(8,128)(2,1)} %copy_dynamic-update-slice_fusion, bf16[4,53,3,336]{3,2,1,0:T(4,128)(2,1)S(1)} %copy.34), kind=kLoop, calls=%fused_computation.9 | loop fusion | flops 12394368 | bytes 8262912 | tf_op jit(solution)/shard_map/concatenate | solution.py:239
  134.0 3.0 %pad = bf16[53,4,32,336]{3,2,0,1:T(8,128)(2,1)} pad(bf16[53,4,29,336]{3,2,0,1:T(8,128)(2,1)S(1)} %maximum_bitcast_fusion, bf16[]{:T(256)} %constant.44.clone.1), padding=0_0x0_0x0_3x0_0 | pad | bytes 8690306 | tf_op jit(solution)/shard_map/concatenate | solution.py:239
  136.9 9.5 %reshape.116 = bf16[53,4,8,4,336]{4,3,2,0,1:T(4,128)(2,1)} reshape(bf16[53,4,32,336]{3,2,0,1:T(8,128)(2,1)} %pad) | data formatting | bytes 9117696 | tf_op jit(solution)/shard_map/conv_general_dilated | solution.py:203
  146.5 3.9 %slice.20 = bf16[53,4,7,2,336]{4,3,2,0,1:T(2,128)(2,1)S(1)} slice(bf16[53,4,8,4,336]{4,3,2,0,1:T(4,128)(2,1)} %reshape.116), slice={[0:53], [0:4], [1:8], [0:2], [0:336]} | slice | bytes 3988992 | tf_op jit(solution)/shard_map/conv_general_dilated | solution.py:203
  150.3 0.0 copy-start.5
  150.3 0.0 copy-start.11
  150.4 7.8 %fusion.1 = bf16[53,4,8,6,336]{4,3,2,0,1:T(8,128)(2,1)S(1)} fusion(bf16[53,4,7,2,336]{4,3,2,0,1:T(2,128)(2,1)S(1)} %slice.20, bf16[53,4,8,4,336]{4,3,2,0,1:T(4,128)(2,1)} %reshape.116), kind=kLoop, calls=%fused_computation.2 | loop fusion | flops 20514816 | bytes 13391616 | tf_op jit(solution)/shard_map/conv_general_dilated | solution.py:203
  158.2 23.5 %maximum_convert_fusion = bf16[51,32,4,256]{3,1,2,0:T(8,128)(2,1)S(1)} fusion(f32[256]{0:T(256)S(1)} %copy-done.5, pred[32,4]{0,1:T(4,128)(4,1)S(1)} %copy-done.11, bf16[3,3,336,256]{3,2,1,0:T(8,128)(2,1)S(1)} %copy-done, bf16[53,4,8,6,336]{4,3,2,0,1:T(8,128)(2,1)S(1)} %fusion.1), kind=kOutput, calls=%fused_computation.8 | convolution fusion | flops 10113908736 | bytes 11730048 | tf_op jit(solution)/shard_map/conv_general_dilated | solution.py:203
  181.6 4.9 %copy.36 = bf16[51,32,4,256]{3,2,1,0:T(4,128)(2,1)} copy(bf16[51,32,4,256]{3,1,2,0:T(8,128)(2,1)S(1)} %maximum_convert_fusion) | data formatting | bytes 6684672 | tf_op jit(solution)/shard_map/convert_element_type | solution.py:247
  186.6 6.5 %reshape.120 = bf16[51,4,32,256]{3,2,1,0:T(8,128)(2,1)} reshape(bf16[51,32,4,256]{3,2,1,0:T(4,128)(2,1)} %copy.36) | data formatting | bytes 6684672 | tf_op jit(solution)/shard_map/convert_element_type | solution.py:247
  193.0 2.2 %slice_select_fusion = bf16[51,4,27,256]{3,2,1,0:T(8,128)(2,1)S(1)} fusion(bf16[51,4,32,256]{3,2,1,0:T(8,128)(2,1)} %reshape.120, pred[51,27]{1,0:T(8,128)(4,1)S(1)} %broadcast_and_fusion), kind=kLoop, calls=%fused_computation.16 | loop fusion | flops 1410048 | bytes 5641569 | tf_op jit(solution)/shard_map/jit(_where)/select_n | solution.py:219
  195.3 2.8 %copy.46 = bf16[51,4,27,256]{3,1,2,0:T(4,128)(2,1)S(1)} copy(bf16[51,4,27,256]{3,2,1,0:T(8,128)(2,1)S(1)} %slice_select_fusion) | data formatting | bytes 5640192
  198.1 1.8 pad.2.clone
  199.9 0.6 slice.22
  200.5 0.0 copy-start.10
  200.5 3.0 %fusion.6 = bf16[51,4,8,6,256]{4,1,3,2,0:T(4,128)(2,1)S(1)} fusion(bf16[51,4,7,2,256]{4,1,3,2,0:T(4,128)(2,1)S(1)} %slice.22, bf16[51,4,8,4,256]{4,1,3,2,0:T(4,128)(2,1)S(1)} %bitcast.46), kind=kLoop, calls=%fused_computation.10 | loop fusion | flops 15040512 | bytes 9818112 | tf_op jit(solution)/shard_map/conv_general_dilated | solution.py:203
  203.5 7.9 %maximum_convert_fusion.1 = bf16[49,32,4,128]{3,1,2,0:T(8,128)(2,1)S(1)} fusion(bf16[3,3,256,128]{3,2,1,0:T(8,128)(2,1)S(1)} %copy-done.2, bf16[51,4,8,6,256]{4,1,3,2,0:T(4,128)(2,1)S(1)} %fusion.6, f32[128]{0:T(128)S(1)} %copy-done.7, pred[32,4]{0,1:T(4,128)(4,1)S(1)} %copy-done.10), kind=kOutput, calls=%fused_computation.17 | convolution fusion | flops 3702587392 | bytes 7209600 | tf_op jit(solution)/shard_map/conv_general_dilated | solution.py:203
  211.5 0.8 copy.39
  212.3 0.3 slice_select_fusion.1
  212.6 0.3 fusion.34
  212.9 0.0 copy-start.9
  212.9 0.5 pad.4
  213.4 0.4 copy.41
  213.8 0.3 slice.25
  214.1 1.2 maximum_convert_fusion.2
  215.3 0.4 copy.42
  215.8 0.3 fusion.25
  216.1 0.1 copy.43
  216.2 0.7 slice.24
  216.9 0.2 broadcast_in_dim.44
  217.1 0.8 broadcast_in_dim.45
  218.0 0.4 pad_maximum_fusion
  218.4 1.6 copy.44
  (25 shorter events, 0.1 us)
Async XLA Ops:
  0.0 158.2 %copy-start = (bf16[3,3,336,256]{3,2,1,0:T(8,128)(2,1)S(1)}, bf16[3,3,336,256]{3,2,1,0:T(8,128)(2,1)}, u32[]{:S(2)}) copy-start(bf16[3,3,336,256]{3,2,1,0:T(8,128)(2,1)} %param.12) | copy-start | bytes 4644868
  107.6 21.1 %collective-permute-start = (bf16[4,53,3,336]{3,0,2,1:T(4,128)(2,1)S(1)}, bf16[4,53,3,336]{3,0,2,1:T(4,128)(2,1)S(1)}, u32[]{:S(2)}, u32[]{:S(2)}) collective-permute-start(bf16[4,53,3,336]{3,0,2,1:T(4,128)(2,1)S(1)} %copy.33), channel_id=1, source_target_pairs={{0,2},{2,4},{4,6},{6,8},{8,10},{10,12},{12,14},{1,3},{3,5},{5,7},{... | collective-permute-start | bytes 1282184 | tf_op jit(solution)/shard_map/ppermute | solution.py:241
  111.0 17.9 %collective-permute-start.1 = (bf16[4,53,2,336]{3,2,1,0:T(2,128)(2,1)S(1)}, bf16[4,53,2,336]{3,2,1,0:T(2,128)(2,1)S(1)}, u32[]{:S(2)}, u32[]{:S(2)}) collective-permute-start(bf16[4,53,2,336]{3,2,1,0:T(2,128)(2,1)S(1)} %slice.19), channel_id=1, source_target_pairs={{2,0},{4,2},{6,4},{8,6},{10,8},{12,10},{14,12},{3,1},{5,3},{7,5},{... | collective-permute-start | bytes 854792 | tf_op jit(solution)/shard_map/ppermute | solution.py:243
  150.3 7.8 %copy-start.5 = (f32[256]{0:T(256)S(1)}, f32[256]{0:T(256)}, u32[]{:S(2)}) copy-start(f32[256]{0:T(256)} %param.13) | copy-start | bytes 3076
  150.3 7.8 %copy-start.11 = (pred[32,4]{0,1:T(4,128)(4,1)S(1)}, pred[32,4]{0,1:T(4,128)(4,1)}, u32[]{:S(2)}) copy-start(pred[32,4]{0,1:T(4,128)(4,1)} %constant.60) | copy-start | bytes 388
  200.4 3.1 %copy-start.2 = (bf16[3,3,256,128]{3,2,1,0:T(8,128)(2,1)S(1)}, bf16[3,3,256,128]{3,2,1,0:T(8,128)(2,1)}, u32[]{:S(2)}) copy-start(bf16[3,3,256,128]{3,2,1,0:T(8,128)(2,1)} %param.14) | copy-start | bytes 1769476
  200.4 3.1 %copy-start.7 = (f32[128]{0:T(128)S(1)}, f32[128]{0:T(128)}, u32[]{:S(2)}) copy-start(f32[128]{0:T(128)} %param.15) | copy-start | bytes 1540
  200.5 3.1 %copy-start.10 = (pred[32,4]{0,1:T(4,128)(4,1)S(1)}, pred[32,4]{0,1:T(4,128)(4,1)}, u32[]{:S(2)}) copy-start(pred[32,4]{0,1:T(4,128)(4,1)} %constant.59) | copy-start | bytes 388
  212.9 1.2 copy-start.3
  212.9 1.2 copy-start.6
  212.9 1.2 copy-start.9
  214.1 1.7 copy-start.4
  214.1 1.7 copy-start.8
  218.0 1.9 copy-start.1
where the time goes:
time: 219 us; the launch traced here: 220 us
  Pallas kernels  95.5 us (44%)
  local copies, waits for them, and re-layouts  52.5 us (24%)
  matrix products  32.9 us (15%)
  other arithmetic  19.2 us (9%)
  waiting for transfers between devices  13.5 us (6%)
  starting transfers between devices  5.84 us (3%)
    pallas_call x1, Pallas kernels, exchange(): pl.pallas_call(functools.partial(exchange_kernel, R, C), out_shape=(jax.S...  95.5 us
    conv_general_dilated x3, matrix products, conv_valid(): lax.conv_general_dilated(inputs, kernel, (stride, stride), 'VALID', dimen...  32.6 us
    conv_general_dilated x5, local copies, waits for them, and re-layouts, conv_valid(): lax.conv_general_dilated(inputs, kernel, (stride, stride), 'VALID', dimen...  14.6 us
    ppermute x1, waiting for transfers between devices, local(): lax.ppermute(stacked[:, :, -ABOVE:], 'cols', right)  13.5 us
    convert_element_type x2, local copies, waits for them, and re-layouts, local(): jax.nn.relu(conv_valid(padded, joined_weight, 1) + joined_bias)  11.4 us
    conv_general_dilated x2, other arithmetic, conv_valid(): lax.conv_general_dilated(inputs, kernel, (stride, stride), 'VALID', dimen...  10.8 us
    unnamed x26, local copies, waits for them, and re-layouts  6.4 us
    concatenate x1, other arithmetic, local(): jnp.concatenate([lax.ppermute(stacked[:, :, -ABOVE:], 'cols', right), sta...  5.01 us
  transfers between devices with their start and end apart: 2, of which 1 were waited for; matrix products, arithmetic and copies ran while one was open for 1% of the time, Pallas kernels for 0%

commit v1 on v0

--- a/solution.py
+++ b/solution.py
@@ -196,27 +196,139 @@
     )(lidar_map, cam)
     cams = cams.reshape(blocks, frames, rows, cam_width, cam_channels)
     cams = cams.transpose(1, 2, 0, 3, 4).reshape(frames, rows, width, cam_channels)
-    return jnp.concatenate([tile, cams], axis=-1)
-
-
-def conv_valid(inputs, kernel, stride):
-    return lax.conv_general_dilated(
-        inputs,
-        kernel,
-        (stride, stride),
-        "VALID",
-        dimension_numbers=("NHWC", "HWIO", "NHWC"),
-        preferred_element_type=jnp.float32,
-    )
-
-
-def inside(values, above, left, height, width):
-    R, C = lax.axis_size("rows"), lax.axis_size("cols")
-    row = lax.axis_index("rows") * height - above + jnp.arange(values.shape[1])
-    col = lax.axis_index("cols") * width - left + jnp.arange(values.shape[2])
-    rows_in = (row >= 0) & (row < R * height)
-    cols_in = (col >= 0) & (col < C * width)
-    return jnp.where((rows_in[:, None] & cols_in[None, :])[None, :, :, None], values, 0)
+    return tile, cams
+
+
+EDGE = 8
+
+
+def with_edges(cells):
+    C = lax.axis_size("cols")
+    right = [(i, i + 1) for i in range(C - 1)]
+    left = [(i + 1, i) for i in range(C - 1)]
+    before = jnp.swapaxes(cells[:, :, -ABOVE:], 1, 2)
+    after = jnp.swapaxes(cells[:, :, :BELOW], 1, 2)
+    before = lax.ppermute(before, "cols", right)
+    after = lax.ppermute(after, "cols", left)
+    before = jnp.pad(jnp.swapaxes(before, 1, 2), ((0, 0), (0, 1), (EDGE - ABOVE, 0), (0, 0)))
+    after = jnp.pad(jnp.swapaxes(after, 1, 2), ((0, 0), (1, 0), (0, EDGE - BELOW), (0, 0)))
+    edge = before + after
+    cells = jnp.pad(cells, ((0, 0), (0, 1), (0, 0), (0, 0)))
+    joint = jnp.concatenate([edge, cells], axis=2)
+    return joint.reshape(joint.shape[0], joint.shape[1] * joint.shape[2], joint.shape[3])
+
+
+def encode_kernel(
+    R, C, span, height,
+    lidar, cam, wj, bj, wb, bb, wd, bd, wp, bp, out, y, joined, block,
+):
+    width = span - EDGE
+    lidar_channels = lidar.shape[2]
+    r, c = lax.axis_index("rows"), lax.axis_index("cols")
+    f32 = jnp.float32
+
+    def dot(a, b):
+        return jnp.dot(a, b, preferred_element_type=f32)
+
+    def rows_at(start, count):
+        return pl.ds(pl.multiple_of(start * span, span), count * span)
+
+    def shifted(row, count, lanes):
+        base = pl.multiple_of(row * span, 8)
+        size = count * span
+        before = pltpu.roll(y[0, pl.ds(base, size + 8), :lanes], 1, 0)[8:]
+        after = pltpu.roll(y[2, pl.ds(base + 8, size + 8), :lanes], size + 7, 0)[:size]
+        return before + y[1, pl.ds(base + 8, size), :lanes] + after
+
+    def masked(values, row, first, wraps):
+        shape = values.shape
+        p = lax.broadcasted_iota(jnp.int32, shape, 0) + row * span
+        i, j = p // span, p % span
+        if wraps:
+            over = j < EDGE - ABOVE
+            i = jnp.where(over, i - 1, i)
+            j = jnp.where(over, j + span, j)
+        i = i + (r * height - first)
+        j = j + (c * width - EDGE)
+        ok = (i >= 0) & (i < R * height) & (j >= 0) & (j < C * width)
+        return jnp.where(ok, values, 0.0)
+
+    joined_rows, block_rows = height + 4, height + 1
+
+    def steps(rows, limit):
+        return max(d for d in range(1, limit + 1) if rows % d == 0)
+
+    n1 = steps(joined_rows, 13)
+
+    @pl.loop(0, joined_rows // n1)
+    def _(t):
+        row = t * n1
+        for dj in range(3):
+            total = None
+            for di in range(3):
+                at = rows_at(row + di, n1)
+                term = dot(lidar[0, at, :], wj[di, dj, :lidar_channels, :])
+                term += dot(cam[0, at, :], wj[di, dj, lidar_channels:, :])
+                total = term if total is None else total + term
+            y[dj, pl.ds(pl.multiple_of(row * span + 8, 8), n1 * span), :] = total
+
+    @pl.loop(0, joined_rows // n1)
+    def _(t):
+        row = t * n1
+        values = jnp.maximum(shifted(row, n1, y.shape[2]) + bj[...], 0.0)
+        joined[rows_at(row, n1), :] = masked(values, row, 2, True).astype(joined.dtype)
+
+    n2 = steps(block_rows + 1, 10)
+    mid = wb.shape[3]
+
+    @pl.loop(0, (block_rows + 1) // n2)
+    def _(t):
+        row = t * n2
+        for dj in range(3):
+            total = None
+            for di in range(3):
+                term = dot(joined[rows_at(row + di, n2), :], wb[di, dj])
+                total = term if total is None else total + term
+            y[dj, pl.ds(pl.multiple_of(row * span + 8, 8), n2 * span), :mid] = total
+
+    m2 = steps(block_rows, 7)
+
+    @pl.loop(0, block_rows // m2)
+    def _(t):
+        row = t * m2
+        values = jnp.maximum(shifted(row, m2, mid) + bb[...], 0.0)
+        values = masked(values, row, 1, False).astype(block.dtype)
+        block[pl.ds(row, m2)] = values.reshape(m2, span, mid)
+
+    half = height // 2
+    n3 = steps(half, 8)
+    deep_channels = wd.shape[3]
+
+    @pl.loop(0, half // n3)
+    def _(t):
+        row = t * n3
+        for dj in range(3):
+            total = None
+            for di in range(3):
+                pairs = block[pl.ds(2 * row + (di // 2) * 2, 2 * n3)]
+                pairs = pairs.reshape(n3, 2, span, mid)[:, di % 2]
+                term = dot(pairs.reshape(n3 * span, mid), wd[di, dj])
+                total = term if total is None else total + term
+            y[dj, pl.ds(pl.multiple_of(row * span + 8, 8), n3 * span), :deep_channels] = total
+
+    @pl.loop(0, half // n3)
+    def _(t):
+        row = t * n3
+        deep = jnp.maximum(shifted(row, n3, deep_channels) + bd[...], 0.0).astype(block.dtype)
+        branch = jnp.maximum(dot(deep, wp[...]) + bp[...], 0.0)
+        odd = lax.broadcasted_iota(jnp.int32, branch.shape, 0) % 2 == 1
+        branch = jnp.where(odd, pltpu.roll(branch, 1, 0), branch)
+        branch = branch.reshape(n3, span, mid)[:, EDGE:].astype(out.dtype)
+        branch = jnp.broadcast_to(branch[:, None], (n3, 2, width, mid))
+        at = pl.ds(2 * row, 2 * n3)
+        out[0, at, :, mid:] = branch.reshape(2 * n3, width, mid)
+        kept = block[pl.ds(2 * row + 1, 2 * n3)].astype(f32)[:, EDGE:]
+        out[0, at, :, :mid] = kept.astype(out.dtype)
 
 
 def local(
@@ -231,30 +343,34 @@
     proj_weight,
     proj_bias,
 ):
-    C = lax.axis_size("cols")
+    R, C = lax.axis_size("rows"), lax.axis_size("cols")
+    frames = lidar_map.shape[0]
     height, width = lidar_map.shape[1] * C, lidar_map.shape[2] // C
-    stacked = exchange(lidar_map, camera_map)
-    right = [(i, i + 1) for i in range(C - 1)]
-    left = [(i + 1, i) for i in range(C - 1)]
-    padded = jnp.concatenate(
-        [
-            lax.ppermute(stacked[:, :, -ABOVE:], "cols", right),
-            stacked,
-            lax.ppermute(stacked[:, :, :BELOW], "cols", left),
+    span = width + EDGE
+    tile, cams = exchange(lidar_map, camera_map)
+    lidar, cam = with_edges(tile), with_edges(cams)
+    wide = max(joined_weight.shape[3], down_weight.shape[3])
+    mid = block_weight.shape[3]
+    weights = [
+        joined_weight, joined_bias[None], block_weight, block_bias[None],
+        down_weight, down_bias[None], proj_weight, proj_bias[None],
+    ]
+    return pl.pallas_call(
+        functools.partial(encode_kernel, R, C, span, height),
+        grid=(frames,),
+        out_shape=jax.ShapeDtypeStruct((frames, height, width, 2 * mid), lidar.dtype),
+        in_specs=[
+            pl.BlockSpec((1,) + lidar.shape[1:], lambda f: (f, 0, 0)),
+            pl.BlockSpec((1,) + cam.shape[1:], lambda f: (f, 0, 0)),
+        ] + [pl.BlockSpec(memory_space=pltpu.VMEM)] * 8,
+        out_specs=pl.BlockSpec((1, height, width, 2 * mid), lambda f: (f, 0, 0, 0)),
+        scratch_shapes=[
+            pltpu.VMEM((3, (height + 4) * span + 16, wide), jnp.float32),
+            pltpu.VMEM(((height + 4) * span, joined_weight.shape[3]), jnp.bfloat16),
+            pltpu.VMEM((height + 2, span, mid), jnp.bfloat16),
         ],
-        axis=2,
-    )
-    joined = jax.nn.relu(conv_valid(padded, joined_weight, 1) + joined_bias).astype(jnp.bfloat16)
-    joined = inside(joined, 2, 2, height, width)
-    block = jax.nn.relu(conv_valid(joined, block_weight, 1) + block_bias).astype(jnp.bfloat16)
-    block = inside(block, 1, 1, height, width)
-    deep = jax.nn.relu(conv_valid(block, down_weight, 2) + down_bias).astype(jnp.bfloat16)
-    branch = jax.nn.relu(
-        jnp.einsum("fijc,cd->fijd", deep, proj_weight, preferred_element_type=jnp.float32)
-        + proj_bias
-    ).astype(jnp.bfloat16)
-    upsampled = jnp.repeat(jnp.repeat(branch, 2, axis=1), 2, axis=2)
-    return jnp.concatenate([block[:, 1:, 1:], upsampled], axis=-1)
+        compiler_params=pltpu.CompilerParams(vmem_limit_bytes=48 << 20),
+    )(lidar, cam, *weights)
 
 
 def solution(mesh):

time: 219 us -> 177 us (0.81)
  Pallas kernels: 95.5 us -> 146 us
  local copies, waits for them, and re-layouts: 52.5 us -> 7.19 us
  matrix products: 32.9 us -> 0 us
  other arithmetic: 19.2 us -> 3.15 us
  starting transfers between devices: 5.84 us -> 11.8 us
  waiting for transfers between devices: 13.5 us -> 8.65 us
    pallas_call x0 -> x1, Pallas kernels: none -> 50.3 us  [local(): pl.pallas_call(functools.partial(encode_kernel, R, C, span, height), grid...]
    conv_general_dilated x3 -> x0, matrix products: 32.6 us -> none  [conv_valid(): lax.conv_general_dilated(inputs, kernel, (stride, stride), 'VALID', dimen...]
    conv_general_dilated x5 -> x0, local copies, waits for them, and re-layouts: 14.6 us -> none  [conv_valid(): lax.conv_general_dilated(inputs, kernel, (stride, stride), 'VALID', dimen...]
    convert_element_type x5 -> x0, local copies, waits for them, and re-layouts: 12.7 us -> none  [the longest x2 11.4 us: local(): jax.nn.relu(conv_valid(padded, joined_weight, 1) + joined_bias)]
    conv_general_dilated x2 -> x0, other arithmetic: 10.8 us -> none  [conv_valid(): lax.conv_general_dilated(inputs, kernel, (stride, stride), 'VALID', dimen...]
    unnamed x26 -> x18, local copies, waits for them, and re-layouts: 6.4 us -> 0.05 us
    ppermute x2 -> x4, starting transfers between devices: 5.84 us -> 11.8 us  [the longest x2 7.08 us: with_edges(): after = lax.ppermute(after, 'cols', left)]
    concatenate x3 -> x1, local copies, waits for them, and re-layouts: 5.84 us -> 0.32 us  [with_edges(): joint = jnp.concatenate([edge, cells], axis=2)]
  transfers between devices with their start and end apart: 2 -> 4, of which waited for: 1 -> 2; matrix products, arithmetic and copies ran while one was open for 1% -> 2% of each run, Pallas kernels for 0% -> 0%
where the time goes in v1:
time: 177 us
  Pallas kernels  146 us (82%)
  starting transfers between devices  11.8 us (7%)
  waiting for transfers between devices  8.65 us (5%)
  local copies, waits for them, and re-layouts  7.19 us (4%)
  other arithmetic  3.15 us (2%)
    pallas_call x1, Pallas kernels, exchange(): pl.pallas_call(functools.partial(exchange_kernel, R, C), out_shape=(jax.S...  95.5 us
    pallas_call x1, Pallas kernels, local(): pl.pallas_call(functools.partial(encode_kernel, R, C, span, height), grid...  50.3 us
    ppermute x2, starting transfers between devices, with_edges(): after = lax.ppermute(after, 'cols', left)  7.08 us
    ppermute x2, waiting for transfers between devices, with_edges(): before = lax.ppermute(before, 'cols', right)  7.03 us
    ppermute x2, starting transfers between devices, with_edges(): before = lax.ppermute(before, 'cols', right)  4.74 us
  transfers between devices with their start and end apart: 4, of which 2 were waited for; matrix products, arithmetic and copies ran while one was open for 2% of the time, Pallas kernels for 0%

profile of v1, /device:TPU:14, one launch (start us, length us, event | category | flops | bytes accessed | tf_op | source)
XLA Modules:
  0.0 176.8 jit_solution(17106896922088030195)
XLA Ops:
  0.0 2.3 %copy.13.cam = bf16[4,96,8,120]{3,2,1,0:T(8,128)(2,1)} copy(bf16[4,96,8,120]{1,3,2,0:T(8,128)(2,1)} %bitcast.33) | data formatting | bytes 1474560 | tf_op jit(solution)/shard_map/reshape | solution.py:179
  2.3 95.5 %shard_map.100 = (bf16[4,53,24,256]{3,2,1,0:T(8,128)(2,1)}, bf16[2,4,53,8,120]{4,3,2,1,0:T(8,128)(2,1)}) custom-call(bf16[4,6,192,256]{3,2,1,0:T(8,128)(2,1)} %lidar.1, bf16[4,96,8,120]{3,2,1,0:T(8,128)(2,1)} %copy.13.cam), custom_call_target="tpu_custom_call" | custom-call | tf_op jit(solution)/shard_map/pallas_call | solution.py:182
  97.7 1.4 slice_bitcast_fusion
  99.1 1.9 %collective-permute-start = (bf16[4,3,53,256]{3,1,2,0:T(4,128)(2,1)S(1)}, bf16[4,3,53,256]{3,1,2,0:T(4,128)(2,1)S(1)}, u32[]{:S(2)}, u32[]{:S(2)}) collective-permute-start(bf16[4,3,53,256]{3,1,2,0:T(4,128)(2,1)S(1)} %slice_bitcast_fusion), channel_id=1, source_target_pairs={{0,2},{2,4},{4,6},{6,8},{8,10},{10,12},{12,14},{1,3},{3,5},{5,7},{... | collective-permute-start | bytes 976904 | tf_op jit(solution)/shard_map/ppermute | solution.py:211
  101.0 2.7 %reshape.17 = bf16[2,4,53,12,80]{4,3,2,1,0:T(8,128)(2,1)S(1)} reshape(bf16[2,4,53,8,120]{4,3,2,1,0:T(8,128)(2,1)} %get-tuple-element.8) | data formatting | bytes 1628160 | tf_op jit(solution)/shard_map/reshape | solution.py:197
  103.7 0.0 copy-start.8
  103.7 0.4 copy.14
  104.1 4.1 %collective-permute-start.3 = (bf16[4,2,53,80]{3,2,1,0:T(8,128)(2,1)S(1)}, bf16[4,2,53,80]{3,2,1,0:T(8,128)(2,1)S(1)}, u32[]{:S(2)}, u32[]{:S(2)}) collective-permute-start(bf16[4,2,53,80]{3,2,1,0:T(8,128)(2,1)S(1)} %slice_bitcast_fusion.3), channel_id=1, source_target_pairs={{2,0},{4,2},{6,4},{8,6},{10,8},{12,10},{14,12},{3,1},{5,3},{7,5},{... | collective-permute-start | bytes 203528 | tf_op jit(solution)/shard_map/ppermute | solution.py:212
  108.2 2.8 %collective-permute-start.2 = (bf16[4,3,53,80]{3,2,1,0:T(8,128)(2,1)S(1)}, bf16[4,3,53,80]{3,2,1,0:T(8,128)(2,1)S(1)}, u32[]{:S(2)}, u32[]{:S(2)}) collective-permute-start(bf16[4,3,53,80]{3,2,1,0:T(8,128)(2,1)S(1)} %slice_bitcast_fusion.2), channel_id=1, source_target_pairs={{0,2},{2,4},{4,6},{6,8},{8,10},{10,12},{12,14},{1,3},{3,5},{5,7},{... | collective-permute-start | bytes 305288 | tf_op jit(solution)/shard_map/ppermute | solution.py:211
  111.0 0.0 copy-done.8
  111.0 0.1 slice_bitcast_fusion.1
  111.2 3.0 %collective-permute-start.1 = (bf16[4,2,53,256]{3,1,2,0:T(2,128)(2,1)S(1)}, bf16[4,2,53,256]{3,1,2,0:T(2,128)(2,1)S(1)}, u32[]{:S(2)}, u32[]{:S(2)}) collective-permute-start(bf16[4,2,53,256]{3,1,2,0:T(2,128)(2,1)S(1)} %slice_bitcast_fusion.1), channel_id=1, source_target_pairs={{2,0},{4,2},{6,4},{8,6},{10,8},{12,10},{14,12},{3,1},{5,3},{7,5},{... | collective-permute-start | bytes 651272 | tf_op jit(solution)/shard_map/ppermute | solution.py:212
  114.2 1.6 collective-permute-done.3
  115.8 7.0 %collective-permute-done.2 = bf16[4,3,53,80]{3,2,1,0:T(8,128)(2,1)S(1)} collective-permute-done((bf16[4,3,53,80]{3,2,1,0:T(8,128)(2,1)S(1)}, bf16[4,3,53,80]{3,2,1,0:T(8,128)(2,1)S(1)}, u32[]{:S(2)}, u32[]{:S(2)}) %collective-permute-start.2) | collective-permute-done | bytes 101792 | tf_op jit(solution)/shard_map/ppermute | solution.py:211
  122.8 0.1 pad_add_fusion.1
  122.9 0.4 fusion.3
  123.3 0.3 copy.15
  123.6 0.0 collective-permute-done.1
  123.7 0.0 collective-permute-done
  123.7 0.4 pad_add_fusion
  124.1 0.0 copy-start
  124.1 0.0 copy-start.1
  124.1 0.0 copy-start.2
  124.1 0.0 copy-start.3
  124.2 0.0 copy-start.4
  124.2 0.0 copy-start.5
  124.2 0.0 copy-start.6
  124.2 0.0 copy-start.7
  124.2 2.3 %fusion.2 = bf16[4,54,32,256]{3,2,1,0:T(8,128)(2,1)} fusion(bf16[4,53,24,256]{3,2,1,0:T(8,128)(2,1)S(1)} %copy-done.8, bf16[4,54,8,256]{3,2,1,0:T(8,128)(2,1)S(1)} %pad_add_fusion), kind=kLoop, calls=%fused_computation.4 | loop fusion | flops 10616832 | bytes 7028736 | tf_op jit(solution)/shard_map/concatenate | solution.py:217
  126.5 0.0 copy-done
  126.5 0.0 copy-done.1
  126.5 0.0 copy-done.2
  126.5 0.0 copy-done.3
  126.5 0.0 copy-done.4
  126.5 0.0 copy-done.5
  126.5 0.0 copy-done.6
  126.5 0.0 copy-done.7
  126.5 50.3 %shard_map.101 = bf16[4,48,24,256]{3,2,1,0:T(8,128)(2,1)} custom-call(bf16[4,1728,256]{2,1,0:T(8,128)(2,1)} %bitcast.28, bf16[4,1728,80]{2,1,0:T(8,128)(2,1)S(1)} %bitcast.23, bf16[3,3,336,256]{3,2,1,0:T(8,128)(2,1)S(1)} %copy-done, f32[1,256]{1,0:T(1,128)S(1)} %bitcast.24, bf16[3,3,256,128]{3,2,1,0:T(8,128)(2,1)S(1)} %copy-done.1, f32[1,128]{1,0:T(1,128)S(1)} %bitcast.26, ...), custom_call_target="tpu_custom_call" | custom-call | tf_op jit(solution)/shard_map/pallas_call | solution.py:358
  (2 shorter events, 0.0 us)
Async XLA Ops:
  99.1 24.5 %collective-permute-start = (bf16[4,3,53,256]{3,1,2,0:T(4,128)(2,1)S(1)}, bf16[4,3,53,256]{3,1,2,0:T(4,128)(2,1)S(1)}, u32[]{:S(2)}, u32[]{:S(2)}) collective-permute-start(bf16[4,3,53,256]{3,1,2,0:T(4,128)(2,1)S(1)} %slice_bitcast_fusion), channel_id=1, source_target_pairs={{0,2},{2,4},{4,6},{6,8},{8,10},{10,12},{12,14},{1,3},{3,5},{5,7},{... | collective-permute-start | bytes 976904 | tf_op jit(solution)/shard_map/ppermute | solution.py:211
  103.7 7.3 %copy-start.8 = (bf16[4,53,24,256]{3,2,1,0:T(8,128)(2,1)S(1)}, bf16[4,53,24,256]{3,2,1,0:T(8,128)(2,1)}, u32[]{:S(2)}) copy-start(bf16[4,53,24,256]{3,2,1,0:T(8,128)(2,1)} %get-tuple-element.7) | copy-start | bytes 7815172
  104.1 11.7 %collective-permute-start.3 = (bf16[4,2,53,80]{3,2,1,0:T(8,128)(2,1)S(1)}, bf16[4,2,53,80]{3,2,1,0:T(8,128)(2,1)S(1)}, u32[]{:S(2)}, u32[]{:S(2)}) collective-permute-start(bf16[4,2,53,80]{3,2,1,0:T(8,128)(2,1)S(1)} %slice_bitcast_fusion.3), channel_id=1, source_target_pairs={{2,0},{4,2},{6,4},{8,6},{10,8},{12,10},{14,12},{3,1},{5,3},{7,5},{... | collective-permute-start | bytes 203528 | tf_op jit(solution)/shard_map/ppermute | solution.py:212
  108.2 14.6 %collective-permute-start.2 = (bf16[4,3,53,80]{3,2,1,0:T(8,128)(2,1)S(1)}, bf16[4,3,53,80]{3,2,1,0:T(8,128)(2,1)S(1)}, u32[]{:S(2)}, u32[]{:S(2)}) collective-permute-start(bf16[4,3,53,80]{3,2,1,0:T(8,128)(2,1)S(1)} %slice_bitcast_fusion.2), channel_id=1, source_target_pairs={{0,2},{2,4},{4,6},{6,8},{8,10},{10,12},{12,14},{1,3},{3,5},{5,7},{... | collective-permute-start | bytes 305288 | tf_op jit(solution)/shard_map/ppermute | solution.py:211
  111.2 12.5 %collective-permute-start.1 = (bf16[4,2,53,256]{3,1,2,0:T(2,128)(2,1)S(1)}, bf16[4,2,53,256]{3,1,2,0:T(2,128)(2,1)S(1)}, u32[]{:S(2)}, u32[]{:S(2)}) collective-permute-start(bf16[4,2,53,256]{3,1,2,0:T(2,128)(2,1)S(1)} %slice_bitcast_fusion.1), channel_id=1, source_target_pairs={{2,0},{4,2},{6,4},{8,6},{10,8},{12,10},{14,12},{3,1},{5,3},{7,5},{... | collective-permute-start | bytes 651272 | tf_op jit(solution)/shard_map/ppermute | solution.py:212
  124.1 2.4 %copy-start = (bf16[3,3,336,256]{3,2,1,0:T(8,128)(2,1)S(1)}, bf16[3,3,336,256]{3,2,1,0:T(8,128)(2,1)}, u32[]{:S(2)}) copy-start(bf16[3,3,336,256]{3,2,1,0:T(8,128)(2,1)} %wj.1) | copy-start | bytes 4644868
  124.1 2.3 %copy-start.1 = (bf16[3,3,256,128]{3,2,1,0:T(8,128)(2,1)S(1)}, bf16[3,3,256,128]{3,2,1,0:T(8,128)(2,1)}, u32[]{:S(2)}) copy-start(bf16[3,3,256,128]{3,2,1,0:T(8,128)(2,1)} %wb.1) | copy-start | bytes 1769476
  124.1 2.3 %copy-start.2 = (bf16[3,3,128,256]{3,2,1,0:T(8,128)(2,1)S(1)}, bf16[3,3,128,256]{3,2,1,0:T(8,128)(2,1)}, u32[]{:S(2)}) copy-start(bf16[3,3,128,256]{3,2,1,0:T(8,128)(2,1)} %wd.1) | copy-start | bytes 1769476
  124.1 2.3 %copy-start.3 = (bf16[256,128]{1,0:T(8,128)(2,1)S(1)}, bf16[256,128]{1,0:T(8,128)(2,1)}, u32[]{:S(2)}) copy-start(bf16[256,128]{1,0:T(8,128)(2,1)} %wp.1) | copy-start | bytes 196612
  124.2 2.3 %copy-start.4 = (f32[256]{0:T(256)S(1)}, f32[256]{0:T(256)}, u32[]{:S(2)}) copy-start(f32[256]{0:T(256)} %param.13) | copy-start | bytes 3076
  124.2 2.3 %copy-start.5 = (f32[256]{0:T(256)S(1)}, f32[256]{0:T(256)}, u32[]{:S(2)}) copy-start(f32[256]{0:T(256)} %param.17) | copy-start | bytes 3076
  124.2 2.3 %copy-start.6 = (f32[128]{0:T(128)S(1)}, f32[128]{0:T(128)}, u32[]{:S(2)}) copy-start(f32[128]{0:T(128)} %param.15) | copy-start | bytes 1540
  124.2 2.3 %copy-start.7 = (f32[128]{0:T(128)S(1)}, f32[128]{0:T(128)}, u32[]{:S(2)}) copy-start(f32[128]{0:T(128)} %param.19) | copy-start | bytes 1540

commit v2 on v1

--- a/solution.py
+++ b/solution.py
@@ -241,17 +241,19 @@
         return before + y[1, pl.ds(base + 8, size), :lanes] + after
 
     def masked(values, row, first, wraps):
-        shape = values.shape
-        p = lax.broadcasted_iota(jnp.int32, shape, 0) + row * span
-        i, j = p // span, p % span
+        flat = values.shape
+        values = values.reshape(flat[0] // span, span, flat[1])
+        i = lax.broadcasted_iota(jnp.int32, values.shape, 0)
+        j = lax.broadcasted_iota(jnp.int32, (1, span, flat[1]), 1)
+        high = R * height - (row + r * height - first)
+        low = high - R * height
         if wraps:
             over = j < EDGE - ABOVE
-            i = jnp.where(over, i - 1, i)
+            i = i - jnp.where(over, 1, 0)
             j = jnp.where(over, j + span, j)
-        i = i + (r * height - first)
         j = j + (c * width - EDGE)
-        ok = (i >= 0) & (i < R * height) & (j >= 0) & (j < C * width)
-        return jnp.where(ok, values, 0.0)
+        ok = (i >= low) & (i < high) & ((j >= 0) & (j < C * width))
+        return jnp.where(ok, values, 0.0).reshape(flat)
 
     joined_rows, block_rows = height + 4, height + 1
 

time: 177 us -> 171 us (0.966)
  Pallas kernels: 146 us -> 139 us
    pallas_call x1, Pallas kernels: 50.3 us -> 43.6 us  [local(): pl.pallas_call(functools.partial(encode_kernel, R, C, span, height), grid...]
where the time goes in v2:
time: 171 us; the launch traced here: 170 us
  Pallas kernels  139 us (81%)
  starting transfers between devices  11.8 us (7%)
  waiting for transfers between devices  8.65 us (5%)
  local copies, waits for them, and re-layouts  7.19 us (4%)
  other arithmetic  3.15 us (2%)
    pallas_call x1, Pallas kernels, exchange(): pl.pallas_call(functools.partial(exchange_kernel, R, C), out_shape=(jax.S...  95.5 us
    pallas_call x1, Pallas kernels, local(): pl.pallas_call(functools.partial(encode_kernel, R, C, span, height), grid...  43.6 us
    ppermute x2, starting transfers between devices, with_edges(): after = lax.ppermute(after, 'cols', left)  7.08 us
    ppermute x2, waiting for transfers between devices, with_edges(): before = lax.ppermute(before, 'cols', right)  7.03 us
    ppermute x2, starting transfers between devices, with_edges(): before = lax.ppermute(before, 'cols', right)  4.74 us
  transfers between devices with their start and end apart: 4, of which 2 were waited for; matrix products, arithmetic and copies ran while one was open for 2% of the time, Pallas kernels for 0%

profile of v2, /device:TPU:14, one launch (start us, length us, event | category | flops | bytes accessed | tf_op | source)
XLA Modules:
  0.0 170.2 jit_solution(4746753590995012574)
XLA Ops:
  0.0 2.3 %copy.13.cam = bf16[4,96,8,120]{3,2,1,0:T(8,128)(2,1)} copy(bf16[4,96,8,120]{1,3,2,0:T(8,128)(2,1)} %bitcast.33) | data formatting | bytes 1474560 | tf_op jit(solution)/shard_map/reshape | solution.py:179
  2.3 95.5 %shard_map.100 = (bf16[4,53,24,256]{3,2,1,0:T(8,128)(2,1)}, bf16[2,4,53,8,120]{4,3,2,1,0:T(8,128)(2,1)}) custom-call(bf16[4,6,192,256]{3,2,1,0:T(8,128)(2,1)} %lidar.1, bf16[4,96,8,120]{3,2,1,0:T(8,128)(2,1)} %copy.13.cam), custom_call_target="tpu_custom_call" | custom-call | tf_op jit(solution)/shard_map/pallas_call | solution.py:182
  97.7 1.4 slice_bitcast_fusion
  99.1 1.9 %collective-permute-start = (bf16[4,3,53,256]{3,1,2,0:T(4,128)(2,1)S(1)}, bf16[4,3,53,256]{3,1,2,0:T(4,128)(2,1)S(1)}, u32[]{:S(2)}, u32[]{:S(2)}) collective-permute-start(bf16[4,3,53,256]{3,1,2,0:T(4,128)(2,1)S(1)} %slice_bitcast_fusion), channel_id=1, source_target_pairs={{0,2},{2,4},{4,6},{6,8},{8,10},{10,12},{12,14},{1,3},{3,5},{5,7},{... | collective-permute-start | bytes 976904 | tf_op jit(solution)/shard_map/ppermute | solution.py:211
  101.0 2.7 %reshape.17 = bf16[2,4,53,12,80]{4,3,2,1,0:T(8,128)(2,1)S(1)} reshape(bf16[2,4,53,8,120]{4,3,2,1,0:T(8,128)(2,1)} %get-tuple-element.8) | data formatting | bytes 1628160 | tf_op jit(solution)/shard_map/reshape | solution.py:197
  103.7 0.0 copy-start.8
  103.7 0.4 copy.14
  104.1 4.1 %collective-permute-start.3 = (bf16[4,2,53,80]{3,2,1,0:T(8,128)(2,1)S(1)}, bf16[4,2,53,80]{3,2,1,0:T(8,128)(2,1)S(1)}, u32[]{:S(2)}, u32[]{:S(2)}) collective-permute-start(bf16[4,2,53,80]{3,2,1,0:T(8,128)(2,1)S(1)} %slice_bitcast_fusion.3), channel_id=1, source_target_pairs={{2,0},{4,2},{6,4},{8,6},{10,8},{12,10},{14,12},{3,1},{5,3},{7,5},{... | collective-permute-start | bytes 203528 | tf_op jit(solution)/shard_map/ppermute | solution.py:212
  108.2 2.8 %collective-permute-start.2 = (bf16[4,3,53,80]{3,2,1,0:T(8,128)(2,1)S(1)}, bf16[4,3,53,80]{3,2,1,0:T(8,128)(2,1)S(1)}, u32[]{:S(2)}, u32[]{:S(2)}) collective-permute-start(bf16[4,3,53,80]{3,2,1,0:T(8,128)(2,1)S(1)} %slice_bitcast_fusion.2), channel_id=1, source_target_pairs={{0,2},{2,4},{4,6},{6,8},{8,10},{10,12},{12,14},{1,3},{3,5},{5,7},{... | collective-permute-start | bytes 305288 | tf_op jit(solution)/shard_map/ppermute | solution.py:211
  111.0 0.0 copy-done.8
  111.0 0.1 slice_bitcast_fusion.1
  111.2 3.0 %collective-permute-start.1 = (bf16[4,2,53,256]{3,1,2,0:T(2,128)(2,1)S(1)}, bf16[4,2,53,256]{3,1,2,0:T(2,128)(2,1)S(1)}, u32[]{:S(2)}, u32[]{:S(2)}) collective-permute-start(bf16[4,2,53,256]{3,1,2,0:T(2,128)(2,1)S(1)} %slice_bitcast_fusion.1), channel_id=1, source_target_pairs={{2,0},{4,2},{6,4},{8,6},{10,8},{12,10},{14,12},{3,1},{5,3},{7,5},{... | collective-permute-start | bytes 651272 | tf_op jit(solution)/shard_map/ppermute | solution.py:212
  114.2 1.6 collective-permute-done.3
  115.8 7.0 %collective-permute-done.2 = bf16[4,3,53,80]{3,2,1,0:T(8,128)(2,1)S(1)} collective-permute-done((bf16[4,3,53,80]{3,2,1,0:T(8,128)(2,1)S(1)}, bf16[4,3,53,80]{3,2,1,0:T(8,128)(2,1)S(1)}, u32[]{:S(2)}, u32[]{:S(2)}) %collective-permute-start.2) | collective-permute-done | bytes 101792 | tf_op jit(solution)/shard_map/ppermute | solution.py:211
  122.8 0.1 pad_add_fusion.1
  122.9 0.4 fusion.3
  123.3 0.3 copy.15
  123.6 0.0 collective-permute-done.1
  123.7 0.0 collective-permute-done
  123.7 0.4 pad_add_fusion
  124.1 0.0 copy-start
  124.1 0.0 copy-start.1
  124.1 0.0 copy-start.2
  124.1 0.0 copy-start.3
  124.2 0.0 copy-start.4
  124.2 0.0 copy-start.5
  124.2 0.0 copy-start.6
  124.2 0.0 copy-start.7
  124.2 2.3 %fusion.2 = bf16[4,54,32,256]{3,2,1,0:T(8,128)(2,1)} fusion(bf16[4,53,24,256]{3,2,1,0:T(8,128)(2,1)S(1)} %copy-done.8, bf16[4,54,8,256]{3,2,1,0:T(8,128)(2,1)S(1)} %pad_add_fusion), kind=kLoop, calls=%fused_computation.4 | loop fusion | flops 10616832 | bytes 7028736 | tf_op jit(solution)/shard_map/concatenate | solution.py:217
  126.5 0.0 copy-done
  126.5 0.0 copy-done.1
  126.5 0.0 copy-done.2
  126.5 0.0 copy-done.3
  126.5 0.0 copy-done.4
  126.5 0.0 copy-done.5
  126.5 0.0 copy-done.6
  126.5 0.0 copy-done.7
  126.5 43.6 %shard_map.101 = bf16[4,48,24,256]{3,2,1,0:T(8,128)(2,1)} custom-call(bf16[4,1728,256]{2,1,0:T(8,128)(2,1)} %bitcast.28, bf16[4,1728,80]{2,1,0:T(8,128)(2,1)S(1)} %bitcast.23, bf16[3,3,336,256]{3,2,1,0:T(8,128)(2,1)S(1)} %copy-done, f32[1,256]{1,0:T(1,128)S(1)} %bitcast.24, bf16[3,3,256,128]{3,2,1,0:T(8,128)(2,1)S(1)} %copy-done.1, f32[1,128]{1,0:T(1,128)S(1)} %bitcast.26, ...), custom_call_target="tpu_custom_call" | custom-call | tf_op jit(solution)/shard_map/pallas_call | solution.py:360
  (2 shorter events, 0.0 us)
Async XLA Ops:
  99.1 24.5 %collective-permute-start = (bf16[4,3,53,256]{3,1,2,0:T(4,128)(2,1)S(1)}, bf16[4,3,53,256]{3,1,2,0:T(4,128)(2,1)S(1)}, u32[]{:S(2)}, u32[]{:S(2)}) collective-permute-start(bf16[4,3,53,256]{3,1,2,0:T(4,128)(2,1)S(1)} %slice_bitcast_fusion), channel_id=1, source_target_pairs={{0,2},{2,4},{4,6},{6,8},{8,10},{10,12},{12,14},{1,3},{3,5},{5,7},{... | collective-permute-start | bytes 976904 | tf_op jit(solution)/shard_map/ppermute | solution.py:211
  103.7 7.3 %copy-start.8 = (bf16[4,53,24,256]{3,2,1,0:T(8,128)(2,1)S(1)}, bf16[4,53,24,256]{3,2,1,0:T(8,128)(2,1)}, u32[]{:S(2)}) copy-start(bf16[4,53,24,256]{3,2,1,0:T(8,128)(2,1)} %get-tuple-element.7) | copy-start | bytes 7815172
  104.1 11.7 %collective-permute-start.3 = (bf16[4,2,53,80]{3,2,1,0:T(8,128)(2,1)S(1)}, bf16[4,2,53,80]{3,2,1,0:T(8,128)(2,1)S(1)}, u32[]{:S(2)}, u32[]{:S(2)}) collective-permute-start(bf16[4,2,53,80]{3,2,1,0:T(8,128)(2,1)S(1)} %slice_bitcast_fusion.3), channel_id=1, source_target_pairs={{2,0},{4,2},{6,4},{8,6},{10,8},{12,10},{14,12},{3,1},{5,3},{7,5},{... | collective-permute-start | bytes 203528 | tf_op jit(solution)/shard_map/ppermute | solution.py:212
  108.2 14.6 %collective-permute-start.2 = (bf16[4,3,53,80]{3,2,1,0:T(8,128)(2,1)S(1)}, bf16[4,3,53,80]{3,2,1,0:T(8,128)(2,1)S(1)}, u32[]{:S(2)}, u32[]{:S(2)}) collective-permute-start(bf16[4,3,53,80]{3,2,1,0:T(8,128)(2,1)S(1)} %slice_bitcast_fusion.2), channel_id=1, source_target_pairs={{0,2},{2,4},{4,6},{6,8},{8,10},{10,12},{12,14},{1,3},{3,5},{5,7},{... | collective-permute-start | bytes 305288 | tf_op jit(solution)/shard_map/ppermute | solution.py:211
  111.2 12.5 %collective-permute-start.1 = (bf16[4,2,53,256]{3,1,2,0:T(2,128)(2,1)S(1)}, bf16[4,2,53,256]{3,1,2,0:T(2,128)(2,1)S(1)}, u32[]{:S(2)}, u32[]{:S(2)}) collective-permute-start(bf16[4,2,53,256]{3,1,2,0:T(2,128)(2,1)S(1)} %slice_bitcast_fusion.1), channel_id=1, source_target_pairs={{2,0},{4,2},{6,4},{8,6},{10,8},{12,10},{14,12},{3,1},{5,3},{7,5},{... | collective-permute-start | bytes 651272 | tf_op jit(solution)/shard_map/ppermute | solution.py:212
  124.1 2.4 %copy-start = (bf16[3,3,336,256]{3,2,1,0:T(8,128)(2,1)S(1)}, bf16[3,3,336,256]{3,2,1,0:T(8,128)(2,1)}, u32[]{:S(2)}) copy-start(bf16[3,3,336,256]{3,2,1,0:T(8,128)(2,1)} %wj.1) | copy-start | bytes 4644868
  124.1 2.3 %copy-start.1 = (bf16[3,3,256,128]{3,2,1,0:T(8,128)(2,1)S(1)}, bf16[3,3,256,128]{3,2,1,0:T(8,128)(2,1)}, u32[]{:S(2)}) copy-start(bf16[3,3,256,128]{3,2,1,0:T(8,128)(2,1)} %wb.1) | copy-start | bytes 1769476
  124.1 2.3 %copy-start.2 = (bf16[3,3,128,256]{3,2,1,0:T(8,128)(2,1)S(1)}, bf16[3,3,128,256]{3,2,1,0:T(8,128)(2,1)}, u32[]{:S(2)}) copy-start(bf16[3,3,128,256]{3,2,1,0:T(8,128)(2,1)} %wd.1) | copy-start | bytes 1769476
  124.1 2.3 %copy-start.3 = (bf16[256,128]{1,0:T(8,128)(2,1)S(1)}, bf16[256,128]{1,0:T(8,128)(2,1)}, u32[]{:S(2)}) copy-start(bf16[256,128]{1,0:T(8,128)(2,1)} %wp.1) | copy-start | bytes 196612
  124.2 2.3 %copy-start.4 = (f32[256]{0:T(256)S(1)}, f32[256]{0:T(256)}, u32[]{:S(2)}) copy-start(f32[256]{0:T(256)} %param.13) | copy-start | bytes 3076
  124.2 2.3 %copy-start.5 = (f32[256]{0:T(256)S(1)}, f32[256]{0:T(256)}, u32[]{:S(2)}) copy-start(f32[256]{0:T(256)} %param.17) | copy-start | bytes 3076
  124.2 2.3 %copy-start.6 = (f32[128]{0:T(128)S(1)}, f32[128]{0:T(128)}, u32[]{:S(2)}) copy-start(f32[128]{0:T(128)} %param.15) | copy-start | bytes 1540
  124.2 2.3 %copy-start.7 = (f32[128]{0:T(128)S(1)}, f32[128]{0:T(128)}, u32[]{:S(2)}) copy-start(f32[128]{0:T(128)} %param.19) | copy-start | bytes 1540
